TPU v7x, 32 devices: a whole 2x2x4 slice. The times are simulated.
32 devices in a mesh: grp: 2 (over x), layer: 4 (over z), feat: 4 (over y, core).
Axes of the slice: x: 2, y: 2, z: 4, core: 2. Of those that a mesh axis runs over, the one named last changes fastest.
Arguments:
- inputs: bfloat16 [4, 512, 2304], P('layer', ('grp', 'feat')), may hold values from -6 to 6
- targets: bfloat16 [512, 4, 2304], P(('grp', 'feat'), None, 'layer'), may hold values from -6 to 6
- enc_weight: bfloat16 [4, 2304, 8192], P('layer', None, 'feat'), may hold values from -0.125 to 0.125
- enc_bias: float32 [4, 8192], P('layer', 'feat'), may hold values from -3 to 3
- dec_weight: bfloat16 [10, 8192, 2304], P(None, 'feat', 'layer'), may hold values from -0.0625 to 0.0625
- dec_bias: float32 [4, 2304], P(None, 'layer'), may hold values from -3 to 3
Outputs:
- enc_grad: bfloat16 [4, 2304, 8192], P('layer', 'grp', 'feat')
- enc_bias_grad: float32 [4, 8192], P('layer', 'feat')
- dec_grad: bfloat16 [10, 8192, 2304], P('grp', 'feat', 'layer')
- dec_bias_grad: float32 [4, 2304], P(None, 'layer')
All inputs are finite; a program needn't handle non-finite values.
Results may differ from a plain program's by a relative error of at most 0.019.
Values may be sent and summed in bfloat16 or wider, within the bound.
A program may use at most 128 MiB of HBM per device.

v0:
```python
import jax
import jax.numpy as jnp
from jax import lax
from jax.sharding import PartitionSpec as P


def pair_list(count):
    return [(source, target) for source in range(count) for target in range(source, count)]


def per_device(inputs, targets, enc_weight, enc_bias, dec_weight, dec_bias):
    layers = lax.axis_size("layer")
    feat_count = lax.axis_size("feat")
    group_count = lax.axis_size("grp")
    pairs = pair_list(layers)
    tok_dev, width = inputs.shape[1], inputs.shape[2]
    group_tokens = tok_dev * feat_count
    total_tokens = group_tokens * group_count
    block = dec_weight.shape[2]
    feats = dec_weight.shape[1]
    rows = lax.all_gather(inputs[0], "feat", axis=0, tiled=True)
    pre = jnp.dot(rows, enc_weight[0], preferred_element_type=jnp.float32) + enc_bias[0]
    acts = jnp.maximum(pre, 0.0).astype(jnp.bfloat16)
    sources = lax.all_gather(acts, "layer", axis=0, tiled=False)

    group = lax.axis_index("grp")
    own_width = width // group_count
    shifts = range(1, group_count)

    def shifted(value, shift):
        return lax.ppermute(
            value, "grp", [(g, (g + shift) % group_count) for g in range(group_count)]
        )

    def with_others(value, axis):
        return jnp.concatenate([value] + [shifted(value, k) for k in shifts], axis=axis)

    def column_block(shift):
        owner = lax.rem(group + shift, group_count)
        return lax.dynamic_slice_in_dim(rows, owner * own_width, own_width, axis=1)

    all_columns = jnp.concatenate(
        [column_block(0)] + [shifted(column_block(k), k) for k in shifts], axis=0
    )
    all_sources = with_others(sources, 1)

    def decode_target(target):
        total = jnp.zeros((group_tokens, block), jnp.float32)
        for index, (source, later) in enumerate(pairs):
            if later == target:
                total = total + jnp.dot(
                    sources[source], dec_weight[index], preferred_element_type=jnp.float32
                )
        return total.astype(jnp.bfloat16).reshape(feat_count, tok_dev, block)

    partial = jnp.stack([decode_target(target) for target in range(layers)], axis=1)
    recon = lax.psum_scatter(
        partial.reshape(feat_count * layers * tok_dev, block),
        "feat",
        scatter_dimension=0,
        tiled=True,
    )
    recon = recon.reshape(layers, tok_dev, block).astype(jnp.float32)
    wanted = jnp.swapaxes(targets, 0, 1).astype(jnp.float32)
    errors = recon + dec_bias[:, None, :] - wanted
    dec_bias_grad = lax.psum(jnp.sum(errors, axis=1), ("grp", "feat")) / total_tokens
    derr_own = (errors / total_tokens).astype(jnp.bfloat16)
    gathered = lax.all_gather(
        derr_own.reshape(layers * tok_dev, block), "feat", axis=0, tiled=True
    )
    gathered = gathered.reshape(feat_count, layers, tok_dev, block)
    derr = jnp.stack(
        [gathered[:, target].reshape(group_tokens, block) for target in range(layers)]
    )
    all_errors = with_others(derr, 1)
    per_group = len(pairs) // group_count

    partials = []
    for source in range(layers):
        total = jnp.zeros((group_tokens, feats), jnp.float32)
        for index, (first, target) in enumerate(pairs):
            if first == source:
                total = total + jnp.einsum(
                    "rd,fd->rf",
                    derr[target],
                    dec_weight[index],
                    preferred_element_type=jnp.float32,
                )
        partials.append(total.astype(jnp.bfloat16))
    dacts = lax.psum_scatter(
        jnp.concatenate(partials, axis=0), "layer", scatter_dimension=0, tiled=True
    ).astype(jnp.float32)
    dpre = jnp.where(pre > 0, dacts, jnp.zeros_like(dacts))
    enc_bias_grad = lax.psum(jnp.sum(dpre, axis=0), "grp")[None]
    all_dpre = with_others(dpre.astype(jnp.bfloat16), 0)

    starts = [group * per_group for group in range(group_count)]
    chosen_s = jnp.array([[s for s, _ in pairs[a : a + per_group]] for a in starts])
    chosen_t = jnp.array([[t for _, t in pairs[a : a + per_group]] for a in starts])

    def pair_grad(slot):
        left = lax.dynamic_index_in_dim(all_sources, chosen_s[group, slot], 0, False)
        right = lax.dynamic_index_in_dim(all_errors, chosen_t[group, slot], 0, False)
        return jnp.einsum("rf,rd->fd", left, right, preferred_element_type=jnp.float32).astype(
            jnp.bfloat16
        )

    dec_grad = jnp.stack([pair_grad(slot) for slot in range(per_group)])
    enc_grad = jnp.einsum(
        "rd,rf->df", all_columns, all_dpre, preferred_element_type=jnp.float32
    ).astype(jnp.bfloat16)[None]
    return (enc_grad, enc_bias_grad, dec_grad, dec_bias_grad)


def solution(mesh):
    return jax.shard_map(
        per_device,
        mesh=mesh,
        in_specs=(
            P("layer", ("grp", "feat"), None),
            P(("grp", "feat"), None, "layer"),
            P("layer", None, "feat"),
            P("layer", "feat"),
            P(None, "feat", "layer"),
            P(None, "layer"),
        ),
        out_specs=(
            P("layer", "grp", "feat"),
            P("layer", "feat"),
            P("grp", "feat", "layer"),
            P(None, "layer"),
        ),
        check_vma=False,
    )
```

profile of v0, /device:TPU:17, one launch (start us, length us, event | category | flops | bytes accessed | tf_op | source)
XLA Modules:
  0.0 415.9 jit_solution(9382348462270128046)
XLA Ops:
  7.2 0.0 all-gather.8.cloned.1.call-start
  7.2 0.7 all-gather.8.cloned.1.call-update
  7.9 0.0 all-gather.10.cloned.1.call-start
  7.9 20.5 %all-gather.8.cloned.1.call-done = bf16[1,256,2304]{2,1,0:T(8,128)(2,1)} async-done(((bf16[1,64,2304]{2,1,0:T(8,128)(2,1)}), bf16[1,256,2304]{2,1,0:T(8,128)(2,1)}) %all-gather.8.cloned.1.call-update) | async-done | bytes 1179664 | tf_op jit(solution)/shard_map/all_gather | solution.py:21
  28.5 8.3 %maximum_convert_fusion = (bf16[256,2048]{1,0:T(8,128)(2,1)}, f32[256,2048]{1,0:T(8,128)}) fusion(f32[2048]{0:T(1024)} %bitcast.230, bf16[1,2304,2048]{2,1,0:T(8,128)(2,1)} %param.10, bf16[1,256,2304]{2,1,0:T(8,128)(2,1)} %all-gather.8.cloned.1.call-done), kind=kOutput, calls=%fused_computation.91 | convolution fusion | flops 2417491968 | bytes 13770752 | tf_op jit(solution)/shard_map/dot_general | solution.py:22
  36.8 0.0 reduce-scatter.3.cloned.1.call-start
  36.8 78.8 %all-gather.10.cloned.1.call-done = bf16[1024,2048]{1,0:T(8,128)(2,1)} async-done(((bf16[256,2048]{1,0:T(8,128)(2,1)}), bf16[1024,2048]{1,0:T(8,128)(2,1)}) %all-gather.10.cloned.1.call-update) | async-done | bytes 4194320 | tf_op jit(solution)/shard_map/all_gather | solution.py:24
  115.6 2.9 fusion.26
  118.6 0.3 copy-done.9
  118.8 2.5 fusion.101
  121.3 2.5 fusion.104
  123.8 2.5 fusion.110
  126.3 0.2 copy.31
  126.5 2.9 fusion.36
  129.4 0.3 copy-done.10
  129.7 2.5 fusion.95
  132.2 2.5 fusion.113
  134.7 0.2 copy.30
  134.9 2.8 fusion.43
  137.7 2.8 fusion.116
  140.5 0.2 copy.29
  140.7 2.8 fusion.119
  143.5 0.2 copy.28
  143.7 0.3 pad_maximum_fusion.2
  144.0 1.2 copy.32
  145.2 0.0 all-gather.6.cloned.1.call-start
  145.3 26.5 %reduce-scatter.3.cloned.1.call-done = bf16[256,576]{1,0:T(8,128)(2,1)} async-done(((bf16[1024,576]{1,0:T(8,128)(2,1)}), bf16[256,576]{1,0:T(8,128)(2,1)}) %reduce-scatter.3.cloned.1.call-update) | async-done | bytes 294928 | tf_op jit(solution)/shard_map/reduce_scatter | solution.py:57
  171.8 1.8 fusion.147
  173.7 0.2 reduce-scatter.5.cloned.1.call-start
  173.9 18.7 %all-gather.6.cloned.1.call-done = bf16[1024,576]{1,0:T(8,128)(2,1)} async-done(((bf16[256,576]{1,0:T(8,128)(2,1)}), bf16[1024,576]{1,0:T(8,128)(2,1)}) %all-gather.6.cloned.1.call-update) | async-done | bytes 1179664 | tf_op jit(solution)/shard_map/all_gather | solution.py:68
  192.6 1.4 fusion.159
  194.0 2.6 fusion.48
  196.6 2.6 fusion.41
  199.3 2.7 convolution_add_fusion.5
  201.9 2.6 fusion.31
  204.6 2.7 convolution_add_fusion.4
  207.3 2.6 convolution_convert_fusion.6
  209.9 2.6 fusion.16
  212.6 2.7 convolution_add_fusion.2
  215.3 2.7 fusion.17
  217.9 2.7 fusion.18
  220.6 2.3 pad_maximum_fusion
  222.9 1.3 collective-permute-start.2
  224.2 0.3 pad_maximum_fusion.3
  224.5 1.4 copy.38
  225.9 0.3 collective-permute-start.3
  226.2 0.7 constant_dynamic-slice_fusion.4
  245.4 2.4 dynamic-slice_bitcast_fusion.1
  247.7 1.2 collective-permute-start
  248.9 120.8 %psum.15 = f32[4,576]{1,0:T(4,128)S(1)} all-reduce(f32[4,576]{1,0:T(4,128)S(1)} %get-tuple-element.12), channel_id=1, replica_groups=mesh['grp'=2,'layer'=4,'feat'=4] {'grp','feat'}, use_global_device_ids=true, to_apply=%region_5.6 | all-reduce | flops 2304 | bytes 18432 | tf_op jit(solution)/shard_map/psum | solution.py:66
  369.7 0.6 broadcast_multiply_fusion
  370.3 1.7 copy.39
  372.0 1.8 pad_maximum_fusion.1
  373.9 1.5 copy-done.1
  375.4 4.1 fusion.4
  379.5 1.9 fusion.70
  381.4 0.3 fusion.71
  381.7 0.4 collective-permute-start.1
  382.0 4.6 %fusion.6 = bf16[5,2048,576]{1,2,0:T(8,128)(2,1)} fusion(bf16[5,2048,576]{1,2,0:T(8,128)(2,1)} %fusion.4, s32[]{:T(128)S(6)} %select_n.60, bf16[4,256,2048]{2,1,0:T(8,128)(2,1)} %bitcast.225, bf16[4,256,2048]{2,1,0:T(8,128)(2,1)} %collective-permute-done.2, bf16[4,512,576]{2,1,0:T(8,128)(2,1)S(1)} %copy-done.2, s32[]{:T(128)S(6)} %select_n.61), kind=kOutput, calls=%fused_computation.23 | convolution fusion | flops 1213333504 | bytes 11403272 | tf_op jit(solution)/shard_map/rf,rd->fd/dot_general | solution.py:104
  386.6 4.1 fusion.8
  390.7 4.1 fusion.10
  394.8 4.1 fusion.12
  398.9 5.1 %psum.14 = f32[1,2048]{1,0:T(1,128)} all-reduce(f32[1,2048]{1,0:T(1,128)S(1)} %bitcast.223), channel_id=1, replica_groups=mesh['grp'=2,'layer'=4,'feat'=4] {'grp'}, use_global_device_ids=true, to_apply=%region_3.0 | all-reduce | flops 2048 | bytes 16384 | tf_op jit(solution)/shard_map/psum | solution.py:94
  404.0 5.3 %fusion.2 = bf16[1,1152,2048]{2,1,0:T(8,128)(2,1)} fusion(bf16[256,2048]{1,0:T(8,128)(2,1)S(1)} %collective-permute-done.1, bf16[256,2048]{1,0:T(8,128)(2,1)S(1)} %fusion.71, bf16[256,1152]{1,0:T(8,128)(2,1)} %collective-permute-done, bf16[256,1152]{1,0:T(8,128)(2,1)S(1)} %copy-done.4), kind=kOutput, calls=%fused_computation.13 | convolution fusion | flops 2424832000 | bytes 7995392 | tf_op jit(solution)/shard_map/rd,rf->df/dot_general | solution.py:109
  (32 shorter events, 0.1 us)
Async XLA Ops:
  7.2 21.3 %all-gather.8.cloned.1.call-start = ((), (), s32[]{:S(2)}) async-start(), calls=%async_computation.5 | async-start | bytes 1474560 | tf_op jit(solution)/shard_map/all_gather | solution.py:21
  7.9 107.7 %all-gather.10.cloned.1.call-start = ((), (), s32[]{:S(2)}) async-start(), calls=%async_computation.6 | async-start | bytes 5242880 | tf_op jit(solution)/shard_map/all_gather | solution.py:24
  36.8 135.0 %reduce-scatter.3.cloned.1.call-start = ((), (), s32[]{:S(2)}) async-start(), calls=%async_computation.2 | async-start | bytes 1638400 | tf_op jit(solution)/shard_map/reduce_scatter | solution.py:57
  115.6 3.2 copy-start.9
  126.5 3.2 copy-start.10
  144.0 27.8 %copy-start.5 = (bf16[64,4,576]{2,1,0:T(4,128)(2,1)S(1)}, bf16[64,4,576]{2,1,0:T(4,128)(2,1)}, u32[]{:S(2)}) copy-start(bf16[64,4,576]{2,1,0:T(4,128)(2,1)} %param.9) | copy-start | bytes 884740
  144.0 27.8 %copy-start.6 = (f32[4,576]{1,0:T(4,128)S(1)}, f32[4,576]{1,0:T(4,128)}, u32[]{:S(2)}) copy-start(f32[4,576]{1,0:T(4,128)} %param.13) | copy-start | bytes 27652
  145.2 47.3 %all-gather.6.cloned.1.call-start = ((), (), s32[]{:S(2)}) async-start(), calls=%async_computation.3 | async-start | bytes 1638400 | tf_op jit(solution)/shard_map/all_gather | solution.py:68
  173.7 205.8 %reduce-scatter.5.cloned.1.call-start = ((), (), s32[]{:S(2)}) async-start(), calls=%async_computation.4 | async-start | bytes 5242880 | tf_op jit(solution)/shard_map/reduce_scatter | solution.py:90
  222.9 3.3 copy-start.7
  222.9 3.3 copy-start.8
  222.9 150.9 %collective-permute-start.2 = (bf16[4,256,2048]{2,1,0:T(8,128)(2,1)}, bf16[4,256,2048]{2,1,0:T(8,128)(2,1)}, u32[]{:S(2)}, u32[]{:S(2)}) collective-permute-start(bf16[4,256,2048]{2,1,0:T(8,128)(2,1)} %bitcast.224), channel_id=1, source_target_pairs={{0,16},{16,0},{1,17},{17,1},{2,18},{18,2},{3,19},{19,3},{4,20},{20... | collective-permute-start | bytes 12582920 | tf_op jit(solution)/shard_map/ppermute | solution.py:31
  225.9 144.4 %collective-permute-start.3 = (bf16[4,256,576]{1,2,0:T(8,128)(2,1)}, bf16[4,256,576]{1,2,0:T(8,128)(2,1)}, u32[]{:S(2)}, u32[]{:S(2)}) collective-permute-start(bf16[4,256,576]{1,2,0:T(8,128)(2,1)} %copy.38), channel_id=1, source_target_pairs={{0,16},{16,0},{1,17},{17,1},{2,18},{18,2},{3,19},{19,3},{4,20},{20... | collective-permute-start | bytes 3538952 | tf_op jit(solution)/shard_map/ppermute | solution.py:31
  247.7 156.3 %collective-permute-start = (bf16[256,1152]{1,0:T(8,128)(2,1)}, bf16[256,1152]{1,0:T(8,128)(2,1)}, u32[]{:S(2)}, u32[]{:S(2)}) collective-permute-start(bf16[256,1152]{1,0:T(8,128)(2,1)} %get-tuple-element.11), channel_id=1, source_target_pairs={{0,16},{16,0},{1,17},{17,1},{2,18},{18,2},{3,19},{19,3},{4,20},{20... | collective-permute-start | bytes 1769480 | tf_op jit(solution)/shard_map/ppermute | solution.py:31
  372.0 3.4 copy-start.11
  373.8 1.6 copy-start.1
  373.8 5.6 %copy-start.3 = (f32[256,2048]{1,0:T(8,128)S(1)}, f32[256,2048]{1,0:T(8,128)}, u32[]{:S(2)}) copy-start(f32[256,2048]{1,0:T(8,128)} %get-tuple-element.25) | copy-start | bytes 6291460
  379.5 1.9 copy-start
  379.5 2.6 copy-start.2
  381.7 4.9 %copy-start.12 = (bf16[1024,2048]{1,0:T(8,128)(2,1)S(1)}, bf16[1024,2048]{1,0:T(8,128)(2,1)}, u32[]{:S(2)}) copy-start(bf16[1024,2048]{1,0:T(8,128)(2,1)} %all-gather.10.cloned.1.call-done) | copy-start | bytes 12582916
  381.7 22.3 %collective-permute-start.1 = (bf16[256,2048]{1,0:T(8,128)(2,1)S(1)}, bf16[256,2048]{1,0:T(8,128)(2,1)S(1)}, u32[]{:S(2)}, u32[]{:S(2)}) collective-permute-start(bf16[256,2048]{1,0:T(8,128)(2,1)S(1)} %fusion.71), channel_id=1, source_target_pairs={{0,16},{16,0},{1,17},{17,1},{2,18},{18,2},{3,19},{19,3},{4,20},{20... | collective-permute-start | bytes 3145736 | tf_op jit(solution)/shard_map/ppermute | solution.py:31
  394.8 9.3 %copy-start.4 = (bf16[256,1152]{1,0:T(8,128)(2,1)S(1)}, bf16[256,1152]{1,0:T(8,128)(2,1)}, u32[]{:S(2)}) copy-start(bf16[256,1152]{1,0:T(8,128)(2,1)} %get-tuple-element.10) | copy-start | bytes 1769476
Sparse Core Ops, SparseCore 0:
  9.5 18.8 all-gather.7
  36.9 78.6 all-gather.9
  145.3 26.4 reduce-scatter.2
  173.8 18.7 all-gather.5
  223.0 76.8 reduce-scatter.4
where the time goes:
time: 422 us; the launch traced here: 416 us
  waiting for transfers between devices  145 us (34%)
  blocking collectives  126 us (30%)
  matrix products  87.8 us (21%)
  between operations  32.6 us (8%)
  local copies, waits for them, and re-layouts  11.6 us (3%)
  other arithmetic  9.26 us (2%)
    psum x1, blocking collectives, per_device(): lax.psum(jnp.sum(errors, axis=1), ('grp', 'feat')) / total_tokens  121 us
    all_gather x1, waiting for transfers between devices, per_device(): sources = lax.all_gather(acts, 'layer', axis=0, tiled=False)  78.8 us
    dot_general x10, matrix products, decode_target(): jnp.dot(sources[source], dec_weight[index], preferred_element_type=jnp.fl...  26.7 us
    dot_general x10, matrix products, per_device(): jnp.einsum('rd,fd->rf', derr[target], dec_weight[index], preferred_elemen...  26.6 us
    reduce_scatter x1, waiting for transfers between devices, per_device(): lax.psum_scatter(partial.reshape(feat_count * layers * tok_dev, block), '...  26.5 us
    dot_general x5, matrix products, pair_grad(): jnp.einsum('rf,rd->fd', left, right, preferred_element_type=jnp.float32)  20.9 us
    all_gather x1, waiting for transfers between devices, per_device(): rows = lax.all_gather(inputs[0], 'feat', axis=0, tiled=True)  20.5 us
    all_gather x1, waiting for transfers between devices, per_device(): lax.all_gather(derr_own.reshape(layers * tok_dev, block), 'feat', axis=0,...  18.7 us
  transfers between devices with their start and end apart: 9, of which 4 were waited for; matrix products, arithmetic and copies ran while one was open for 8% of the time, Pallas kernels for 0%

commit v1 on v0

v1 whole, which is shorter than its diff:
```python
import functools

import jax
import jax.numpy as jnp
from jax import lax
from jax.experimental import pallas as pl
from jax.experimental.pallas import tpu as pltpu
from jax.sharding import PartitionSpec as P

MESH = pl.DeviceIdType.MESH
BF = jnp.bfloat16
F32 = jnp.float32


def pair_list(count):
    return [(source, target) for source in range(count) for target in range(source, count)]


CHUNKS = 2


def dot_nn(a, b):
    return lax.dot_general(a, b, (((1,), (0,)), ((), ())), preferred_element_type=F32)


def dot_nt(a, b):
    return lax.dot_general(a, b, (((1,), (1,)), ((), ())), preferred_element_type=F32)


def dot_tn(a, b):
    return lax.dot_general(a, b, (((0,), (0,)), ((), ())), preferred_element_type=F32)


def rdma(src, dst, ssem, rsem, dev):
    return pltpu.make_async_remote_copy(
        src_ref=src, dst_ref=dst, send_sem=ssem, recv_sem=rsem, device_id=dev, device_id_type=MESH
    )


def kernel(cfg, *refs):
    (L, F, C, B, D, feats, width, cw, per, total, ranges, turned) = cfg
    if not turned:
        refs = refs[:18] + (None,) + refs[18:]
    (inp, tgt, ew, eb, dw, db, eg_o, ebg_o, dg_o, dbg_o,
     w_v, ew_v, acts, rows_v, cols_o, cols_t, acc, derr, derr_t,
     r1b, r1r, r2r, dpre, og_v, eg_v, dbs, dbr, dbx, ebs, ebr,
     ld_w, ld_ew, ld_in, in_p, in_s, in_r, co, zr_s, zl_s, z_r, x_s, x_r, r1_s, r1_r, r2_s, r2_r,
     ag_p, ag_s, ag_r, dx_s, dx_r, db_s, db_r, dbx_m, eb_m, b_s, b_r, dp_s, dp_r, og_m, eg_m) = refs
    g = lax.axis_index("grp")
    l = lax.axis_index("layer")
    f = lax.axis_index("feat")
    Q = feats // cw
    R = F * B
    n = C * R
    H = F // 2
    half = D // 2
    core = lax.rem(f, 2)
    chip = f // 2
    sib = f + 1 - 2 * core
    other = 1 - g
    xdev, sdev = (other, l, f), (g, l, sib)
    rdev, ldev = (g, l + 1, f), (g, l - 1, f)
    has_l, has_r = l > 0, l < L - 1

    def peer(k):
        j = lax.rem(chip + k, H)
        return j, 2 * j + core

    def by_group(which, values):
        return jnp.where(which == 0, values[0], values[1])

    def pair(s, t):
        return s * L - (s * (s - 1)) // 2 + t - s

    def brow(idx, n):
        return pl.ds(pl.multiple_of(idx * n, n), n)

    def need_s(h, s):
        return jnp.logical_and(s >= by_group(h, ranges[0]), s <= by_group(h, ranges[1]))

    def need_t(h, t):
        return jnp.logical_and(t >= by_group(h, ranges[2]), t <= by_group(h, ranges[3]))

    lin = [pltpu.make_async_copy(inp.at[0, pl.ds(c * B, B), :], rows_v.at[brow(c * F + f, B), :], ld_in.at[c])
           for c in range(C)]
    for cp in lin:
        cp.start()
    lew = [pltpu.make_async_copy(ew.at[0, :, pl.ds(q * cw, cw)], ew_v.at[q, pl.ds(0, D), :], ld_ew.at[q])
           for q in range(Q)]
    for cp in lew:
        cp.start()
    lw = [pltpu.make_async_copy(dw.at[p], w_v.at[p], ld_w.at[p]) for p in range(2 * per)]
    for cp in lw:
        cp.start()

    bar = pltpu.get_barrier_semaphore()
    pl.semaphore_signal(bar, inc=1, device_id=xdev, device_id_type=MESH)
    for k in range(1, F):
        pl.semaphore_signal(bar, inc=1, device_id=(g, l, lax.rem(f + k, F)), device_id_type=MESH)

    @pl.when(has_l)
    def _():
        pl.semaphore_signal(bar, inc=1, device_id=ldev, device_id_type=MESH)

    @pl.when(has_r)
    def _():
        pl.semaphore_signal(bar, inc=1, device_id=rdev, device_id_type=MESH)

    pl.semaphore_wait(bar, F + has_l.astype(jnp.int32) + has_r.astype(jnp.int32))

    def row_block(c, owner):
        return rows_v.at[brow(c * F + owner, B), :]

    for c in range(C):
        lin[c].wait()
        mine = row_block(c, f)
        for k in range(1, H):
            _, dev = peer(k)
            rdma(mine, mine, in_p.at[c, k], in_r.at[c, f], (g, l, dev)).start()
        rdma(mine, mine, in_s.at[c, f], in_r.at[c, f], sdev).start()
    acc[...] = jnp.zeros_like(acc)
    dbs[...] = jnp.zeros_like(dbs)
    ebs[...] = jnp.zeros_like(ebs)
    for c in range(C):
        for k in range(1, H):
            _, dev = peer(k)
            blk = row_block(c, dev)
            rdma(blk, blk, in_p.at[c, k], in_r.at[c, dev], sdev).wait_recv()
            rdma(blk, blk, in_s.at[c, dev], in_r.at[c, dev], sdev).start()
        for j in range(H):
            own = 2 * j + 1 - core
            blk = row_block(c, own)
            rdma(blk, blk, in_s.at[c, own], in_r.at[c, own], sdev).wait_recv()

    def cols_copy():
        cols = pl.ds(pl.multiple_of(other * half, half), half)
        return rdma(rows_v.at[:, cols], cols_o, co.at[0], co.at[1], xdev)

    cols_copy().start()

    def act_ref(c, s, q):
        return acts.at[s, q, pl.ds(c * R, R), :]

    def z_right(c, s, q):
        blk = act_ref(c, s, q)
        return rdma(blk, blk, zr_s.at[c, s, q], z_r.at[c, s, q], rdev)

    def z_left(c, s, q):
        blk = act_ref(c, s, q)
        return rdma(blk, blk, zl_s.at[c, s, q], z_r.at[c, s, q], ldev)

    def x_copy(c, s, q):
        return rdma(act_ref(c, s, q), acts.at[s, q, pl.ds(n + c * R, R), :], x_s.at[c, s, q], x_r.at[c, s, q], xdev)

    def decode(c, s, q):
        def one(t, carry):
            acc[c, t] += dot_nt(act_ref(c, s, q)[...], w_v[pair(s, t), :, brow(q, cw)])
            return carry

        lax.fori_loop(s, L, one, 0)

    def encode(q, carry):
        pltpu.make_async_copy(
            ew.at[0, :, pl.ds(pl.multiple_of(q * cw, cw), cw)], ew_v.at[q, pl.ds(0, D), :], ld_ew.at[q]
        ).wait()
        bias = eb[:, pl.ds(pl.multiple_of(q * cw, cw), cw)]
        pre = dot_nn(rows_v[...], ew_v[q, pl.ds(0, D), :]) + bias
        acts[l, q, pl.ds(0, n), :] = jnp.maximum(pre, 0.0).astype(BF)
        send_own(0, q)
        return carry

    def send_own(c, q):
        @pl.when(has_r)
        def _():
            z_right(c, l, q).start()

        @pl.when(has_l)
        def _():
            z_left(c, l, q).start()

        @pl.when(need_s(other, l))
        def _():
            x_copy(c, l, q).start()

    lax.fori_loop(0, Q, encode, 0)
    for cp in lw:
        cp.wait()

    def decode_own(c):
        def own(q, carry):
            decode(c, l, q)
            return carry

        lax.fori_loop(0, Q, own, 0)

    def arrive(c, i):
        k = 1 + i // Q
        q = lax.rem(i, Q)

        def take(s, relay, on):
            blk = act_ref(c, s, q)
            rdma(blk, blk, x_s.at[c, s, q], z_r.at[c, s, q], xdev).wait_recv()

            @pl.when(on)
            def _():
                relay(c, s, q).start()

            @pl.when(need_s(other, s))
            def _():
                x_copy(c, s, q).start()

            decode(c, s, q)

        @pl.when(l - k >= 0)
        def _():
            take(l - k, z_right, has_r)

        @pl.when(l + k <= L - 1)
        def _():
            take(l + k, z_left, has_l)

    def arrivals(c, lo, hi):
        def step(i, carry):
            arrive(c, i)
            return carry

        if lo < hi:
            lax.fori_loop(lo, hi, step, 0)

    def derr_block(c, owner):
        return derr.at[:, brow(c * F + owner, B), :]

    def r1_copy(c, j):
        return rdma(r1b.at[c, j], r1r.at[c, j], r1_s.at[c, j], r1_r.at[c, j], sdev)

    def r2_wait(c, k):
        return rdma(r1r.at[c, 0], r2r.at[c, k - 1], r2_s.at[c, k], r2_r.at[c, k], sdev)

    def dx_copy(c, t):
        return rdma(derr.at[t, pl.ds(c * R, R), :], derr.at[t, pl.ds(n + c * R, R), :], dx_s.at[c, t], dx_r.at[c, t], xdev)

    def mid_pack(c):
        for k in range(1, H + 1):
            j = lax.rem(chip + k, H)
            rows = brow(2 * j + 1 - core, B)
            for t in range(L):
                r1b[c, j, t] = acc[c, t, rows, :].astype(BF)
            r1_copy(c, j).start()

    def mid_sum(c):
        for k in range(1, H):
            j, dev = peer(k)
            r1_copy(c, j).wait_recv()
            for t in range(L):
                r1r[c, j, t] = (acc[c, t, brow(dev, B), :] + r1r[c, j, t].astype(F32)).astype(BF)
            rdma(r1r.at[c, j], r2r.at[c, H - k - 1], r2_s.at[c, k], r2_r.at[c, H - k], (g, l, dev)).start()
        r1_copy(c, chip).wait_recv()
        for t in range(L):
            acc[c, t, brow(f, B), :] += (
                r1r[c, chip, t].astype(F32) + db[pl.ds(t, 1), :] - tgt[t, pl.ds(c * B, B), :].astype(F32)
            )

    def mid_err(c):
        for k in range(1, H):
            r2_wait(c, k).wait_recv()
        for t in range(L):
            err = acc[c, t, brow(f, B), :]
            for k in range(1, H):
                err = err + r2r[c, k - 1, t].astype(F32)
            acc[c, t, brow(f, B), :] = err
            derr[t, brow(c * F + f, B), :] = (err / total).astype(BF)
        mine = derr_block(c, f)
        for k in range(1, H):
            _, dev = peer(k)
            rdma(mine, mine, ag_p.at[c, k], ag_r.at[c, f], (g, l, dev)).start()
        rdma(mine, mine, ag_s.at[c, f], ag_r.at[c, f], sdev).start()
        for t in range(L):
            dbs[pl.ds(t, 1), :] += jnp.sum(acc[c, t, brow(f, B), :], axis=0, keepdims=True)

    def mid_relay(c):
        for k in range(1, H):
            _, dev = peer(k)
            blk = derr_block(c, dev)
            rdma(blk, blk, ag_p.at[c, k], ag_r.at[c, dev], sdev).wait_recv()
            rdma(blk, blk, ag_s.at[c, dev], ag_r.at[c, dev], sdev).start()

    def mid_end(c):
        for j in range(H):
            own = 2 * j + 1 - core
            blk = derr_block(c, own)
            rdma(blk, blk, ag_s.at[c, own], ag_r.at[c, own], sdev).wait_recv()
        for t in range(L):
            @pl.when(need_t(other, t))
            def _():
                dx_copy(c, t).start()

    def slot_ref(slot, c, q):
        return ew_v.at[q, brow(slot * C + c, R), :]

    def partial(c, s, q):
        acc[c, 0, :, pl.ds(0, cw)] = dot_nn(derr[s, pl.ds(c * R, R), :], w_v[pair(s, s), :, brow(q, cw)])

        def one(t, carry):
            acc[c, 0, :, pl.ds(0, cw)] += dot_nn(derr[t, pl.ds(c * R, R), :], w_v[pair(s, t), :, brow(q, cw)])
            return carry

        lax.fori_loop(s + 1, L, one, 0)

    def b_wait(slot, c, q):
        blk = slot_ref(slot, c, q)
        rdma(blk, blk, b_s.at[c, 0, q], b_r.at[c, slot, q], xdev).wait_recv()

    def b_right(c, s, q):
        return rdma(slot_ref(s, c, q), slot_ref(s, c, q), b_s.at[c, s, q], b_r.at[c, s, q], rdev)

    def b_left(c, s, q):
        to = jnp.where(s == l - 1, L, s)
        return rdma(slot_ref(s, c, q), slot_ref(to, c, q), b_s.at[c, s, q], b_r.at[c, to, q], ldev)

    order = [sorted(range(L), key=lambda s: (-abs(s - at), -s if at < L // 2 else s)) for at in range(L)]

    def source_at(k):
        s = jnp.int32(0)
        for at in range(L):
            for j in range(L - 1):
                s = jnp.where(jnp.logical_and(l == at, k == j), order[at][j], s)
        return s

    def send_job(c, i):
        s, q = source_at(i // Q), lax.rem(i, Q)
        partial(c, s, q)
        inner = jnp.where(s > l, has_l, has_r)

        @pl.when(inner)
        def _():
            b_wait(s, c, q)
            acc[c, 0, :, pl.ds(0, cw)] += slot_ref(s, c, q)[...].astype(F32)

        slot_ref(s, c, q)[...] = acc[c, 0, :, pl.ds(0, cw)].astype(BF)

        @pl.when(s > l)
        def _():
            b_right(c, s, q).start()

        @pl.when(s < l)
        def _():
            b_left(c, s, q).start()

    def dp_copy(c, q):
        return rdma(dpre.at[q, pl.ds(c * R, R), :], dpre.at[q, pl.ds(n + c * R, R), :], dp_s.at[c, q], dp_r.at[c, q], xdev)

    def own_job(c, q):
        partial(c, l, q)

        @pl.when(has_l)
        def _():
            b_wait(l, c, q)
            acc[c, 0, :, pl.ds(0, cw)] += slot_ref(l, c, q)[...].astype(F32)

        @pl.when(has_r)
        def _():
            b_wait(L, c, q)
            acc[c, 0, :, pl.ds(0, cw)] += slot_ref(L, c, q)[...].astype(F32)

        grad = jnp.where(act_ref(c, l, q)[...].astype(F32) > 0.0, acc[c, 0, :, pl.ds(0, cw)], 0.0)
        ebs[:, brow(q, cw)] += jnp.sum(grad, axis=0, keepdims=True)
        dpre[q, pl.ds(c * R, R), :] = grad.astype(BF)
        dp_copy(c, q).start()

    starts = [pair(s, s) for s in range(L)]

    def pair_of(p):
        s = jnp.int32(0)
        first = jnp.int32(0)
        for k in range(1, L):
            s = jnp.where(p >= starts[k], k, s)
            first = jnp.where(p >= starts[k], starts[k], first)
        return s, p - first + s

    def og_copy(i):
        slot, q = i // Q, lax.rem(i, Q)
        at = lax.rem(i, 2)
        return pltpu.make_async_copy(og_v.at[at], dg_o.at[slot, :, brow(q, cw)], og_m.at[at])

    def grad_job(i, carry):
        q = lax.rem(i, Q)
        s, t = pair_of(g * per + i // Q)

        @pl.when(i >= 2)
        def _():
            og_copy(i - 2).wait()

        if derr_t is None:
            grad = dot_tn(derr[t], acts[s, q])
        else:
            grad = dot_nn(derr_t[t], acts[s, q])
        og_v[lax.rem(i, 2)] = grad.astype(BF)
        og_copy(i).start()
        return carry

    def eg_copy(q):
        at = lax.rem(q, 2)
        return pltpu.make_async_copy(eg_v.at[at], eg_o.at[0, :, pl.ds(pl.multiple_of(q * cw, cw), cw)], eg_m.at[at])

    def enc_job(q):
        for c in range(C):
            dp_copy(c, q).wait_recv()

        @pl.when(q >= 2)
        def _():
            eg_copy(q - 2).wait()

        eg_v[lax.rem(q, 2)] = dot_nn(cols_t[...], dpre[q]).astype(BF)
        eg_copy(q).start()

    def turn_cols():
        cols = pl.ds(pl.multiple_of(g * half, half), half)
        cols_copy().wait_recv()
        cols_t[:, pl.ds(0, n)] = rows_v[:, cols].T
        cols_t[:, pl.ds(n, n)] = cols_o[...].T

    def wait_others():
        for c in range(C):
            for s in range(L):
                @pl.when(need_s(g, s))
                def _():
                    def one(q, carry):
                        x_copy(c, s, q).wait_recv()
                        return carry

                    lax.fori_loop(0, Q, one, 0)
            for t in range(L):
                @pl.when(need_t(g, t))
                def _():
                    dx_copy(c, t).wait_recv()
        if derr_t is not None:
            for t in range(L):
                @pl.when(need_t(g, t))
                def _():
                    derr_t[t] = derr[t].T

    jobs = per * Q
    steps = (L - 1) * Q

    def cut(i):
        return min(i, steps)

    def send_jobs(c, lo, hi):
        def step(i, carry):
            send_job(c, i)
            return carry

        if lo < hi:
            lax.fori_loop(lo, hi, step, 0)

    decode_own(0)
    arrivals(0, 0, cut(8))
    turn_cols()
    arrivals(0, cut(8), steps)

    def send_second(q, carry):
        send_own(1, q)
        return carry

    lax.fori_loop(0, Q, send_second, 0)
    mid_pack(0)
    mid_sum(0)
    decode_own(1)
    arrivals(1, 0, cut(1))
    mid_err(0)
    arrivals(1, cut(1), cut(4))
    mid_relay(0)
    arrivals(1, cut(4), cut(5))
    mid_end(0)

    def both(i, carry):
        send_job(0, i)
        arrive(1, i + cut(5))
        return carry

    lead = steps - cut(5)
    if lead > 0:
        lax.fori_loop(0, lead, both, 0)
    mid_pack(1)
    send_jobs(0, lead, cut(lead + 1))
    mid_sum(1)
    send_jobs(0, cut(lead + 1), cut(lead + 3))
    mid_err(1)
    for k in range(1, F):
        dev = lax.rem(f + k, F)
        rdma(dbs, dbr.at[F - k], db_s.at[k], db_r.at[F - k], (g, l, dev)).start()
    send_jobs(0, cut(lead + 3), steps)
    mid_relay(1)
    mid_end(1)

    def second(i, carry):
        send_job(1, i)

        @pl.when(jnp.logical_and(i >= 1, i < 1 + Q))
        def _():
            own_job(0, i - 1)

        base = 2 * (i - wait_at)

        @pl.when(i == wait_at)
        def _():
            wait_others()

        lax.fori_loop(jnp.minimum(jnp.maximum(base, 0), jobs), jnp.minimum(jnp.maximum(base + 2, 0), jobs), grad_job, 0)
        return carry

    wait_at = min(3, steps - 1)
    lax.fori_loop(0, steps, second, 0)
    for q in range(max(steps - 1, 0), Q):
        own_job(0, jnp.int32(q))
    lax.fori_loop(min(jobs, 2 * (steps - wait_at)), jobs, grad_job, 0)

    sums = dbs[...]
    for k in range(1, F):
        rdma(dbs, dbr.at[k], db_s.at[k], db_r.at[k], sdev).wait_recv()
        sums = sums + dbr[k]
    dbx[0] = sums
    dbx_copy = rdma(dbx.at[0], dbx.at[1], dbx_m.at[0], dbx_m.at[1], xdev)
    dbx_copy.start()

    def last(q, carry):
        own_job(1, q)

        @pl.when(q >= 1)
        def _():
            enc_job(q - 1)

        return carry

    lax.fori_loop(0, Q, last, 0)
    eb_copy = rdma(ebs, ebr, eb_m.at[0], eb_m.at[1], xdev)
    eb_copy.start()
    enc_job(jnp.int32(Q - 1))
    dbx_copy.wait()
    dbg_o[...] = (dbx[0] + dbx[1]) / total
    eb_copy.wait()
    ebg_o[...] = ebs[...] + ebr[...]

    cols_copy().wait_send()
    for i in range(max(0, jobs - 2), jobs):
        og_copy(jnp.int32(i)).wait()
    for q in range(max(0, Q - 2), Q):
        eg_copy(jnp.int32(q)).wait()
    for k in range(1, F):
        rdma(dbs, dbr.at[k], db_s.at[k], db_r.at[k], sdev).wait_send()
    for c in range(C):
        for k in range(1, H):
            mine = row_block(c, f)
            rdma(mine, mine, in_p.at[c, k], in_r.at[c, f], sdev).wait_send()
            r2_wait(c, k).wait_send()
            blk = derr_block(c, f)
            rdma(blk, blk, ag_p.at[c, k], ag_r.at[c, f], sdev).wait_send()
        for j in range(H):
            r1_copy(c, j).wait_send()
            own = 2 * j + core
            blk = row_block(c, own)
            rdma(blk, blk, in_s.at[c, own], in_r.at[c, own], sdev).wait_send()
            blk = derr_block(c, own)
            rdma(blk, blk, ag_s.at[c, own], ag_r.at[c, own], sdev).wait_send()
        for t in range(L):
            @pl.when(need_t(other, t))
            def _():
                dx_copy(c, t).wait_send()

        def drain(q, carry):
            for s in range(L):
                @pl.when(jnp.logical_and(has_r, s <= l))
                def _():
                    z_right(c, s, q).wait_send()

                @pl.when(jnp.logical_and(has_l, s >= l))
                def _():
                    z_left(c, s, q).wait_send()

                @pl.when(need_s(other, s))
                def _():
                    x_copy(c, s, q).wait_send()

                @pl.when(s != l)
                def _():
                    b_right(c, s, q).wait_send()
            dp_copy(c, q).wait_send()
            return carry

        lax.fori_loop(0, Q, drain, 0)


def per_device(chunks, inputs, targets, enc_weight, enc_bias, dec_weight, dec_bias):
    L = lax.axis_size("layer")
    F = lax.axis_size("feat")
    G = lax.axis_size("grp")
    assert G == 2 and F % 2 == 0
    pairs = pair_list(L)
    per = len(pairs) // G
    tok_dev, D = inputs.shape[1], inputs.shape[2]
    feats, width = dec_weight.shape[1], dec_weight.shape[2]
    C = chunks
    B = tok_dev // C
    R = F * B
    n = C * R
    H = F // 2
    total = tok_dev * F * G
    cw = min(512, feats // 2)
    Q = feats // cw
    groups = [pairs[h * per:(h + 1) * per] for h in range(G)]
    ranges = (
        tuple(min(s for s, _ in grp) for grp in groups),
        tuple(max(s for s, _ in grp) for grp in groups),
        tuple(min(t for _, t in grp) for grp in groups),
        tuple(max(t for _, t in grp) for grp in groups),
    )
    turned = n <= 512
    cfg = (L, F, C, B, D, feats, width, cw, per, total, ranges, turned)
    V = pltpu.VMEM
    S = pltpu.SemaphoreType.DMA
    slots = max(D, (L + 1) * n)
    scratch = [
        V((len(pairs), width, feats), BF), V((Q, slots, cw), BF), V((L, Q, 2 * n, cw), BF),
        V((n, D), BF), V((n, D // 2), BF), V((D // 2, 2 * n), BF), V((C, L, R, width), F32),
        V((L, 2 * n, width), BF), *([V((L, width, 2 * n), BF)] if turned else []),
        V((C, H, L, B, width), BF), V((C, H, L, B, width), BF), V((C, H - 1, L, B, width), BF),
        V((Q, 2 * n, cw), BF), V((2, width, cw), BF), V((min(2, Q), D // 2, cw), BF),
        V((L, width), F32), V((F, L, width), F32), V((2, L, width), F32), V((1, feats), F32), V((1, feats), F32),
        S((len(pairs),)), S((Q,)), S((C,)), S((C, H)), S((C, F)), S((C, F)), S((2,)),
        S((C, L, Q)), S((C, L, Q)), S((C, L, Q)), S((C, L, Q)), S((C, L, Q)), S((C, H)), S((C, H)), S((C, H)), S((C, H)),
        S((C, H)), S((C, F)), S((C, F)), S((C, L)), S((C, L)), S((F,)), S((F,)), S((2,)), S((2,)),
        S((C, L, Q)), S((C, L + 1, Q)), S((C, Q)), S((C, Q)), S((2,)), S((2,)),
    ]
    hbm = pl.BlockSpec(memory_space=pl.ANY)
    vm = pl.BlockSpec(memory_space=pltpu.VMEM)
    enc, encb, dec, decb = pl.pallas_call(
        functools.partial(kernel, cfg),
        out_shape=(
            jax.ShapeDtypeStruct((1, D // 2, feats), BF),
            jax.ShapeDtypeStruct((1, feats), F32),
            jax.ShapeDtypeStruct((per, width, feats), BF),
            jax.ShapeDtypeStruct((L, width), F32),
        ),
        in_specs=[hbm, vm, hbm, vm, hbm, vm],
        out_specs=(hbm, vm, hbm, vm),
        scratch_shapes=scratch,
        compiler_params=pltpu.CompilerParams(
            collective_id=0, has_side_effects=True, vmem_limit_bytes=67043328
        ),
        name="transcoder",
    )(inputs, jnp.swapaxes(targets, 0, 1), enc_weight, enc_bias, jnp.swapaxes(dec_weight, 1, 2), dec_bias)
    return enc, encb, jnp.swapaxes(dec, 1, 2), decb


def solution(mesh):
    return jax.shard_map(
        functools.partial(per_device, CHUNKS),
        mesh=mesh,
        in_specs=(
            P("layer", ("grp", "feat"), None),
            P(("grp", "feat"), None, "layer"),
            P("layer", None, "feat"),
            P("layer", "feat"),
            P(None, "feat", "layer"),
            P(None, "layer"),
        ),
        out_specs=(
            P("layer", "grp", "feat"),
            P("layer", "feat"),
            P("grp", "feat", "layer"),
            P(None, "layer"),
        ),
        check_vma=False,
    )
```

time: 422 us -> 186 us (0.44); the launches traced: 416 us -> 186 us
  Pallas kernels: 0 us -> 166 us
  waiting for transfers between devices: 145 us -> 0 us
  blocking collectives: 126 us -> 0 us
  matrix products: 87.8 us -> 0 us
  between operations: 32.6 us -> 0.64 us
  other arithmetic: 9.26 us -> 0 us
  local copies, waits for them, and re-layouts: 11.6 us -> 19.1 us
    pallas_call x0 -> x1, Pallas kernels: none -> 166 us  [per_device(): pl.pallas_call(functools.partial(kernel, cfg), out_shape=(jax.ShapeDtypeS...]
    psum x2 -> x0, blocking collectives: 126 us -> none  [the longest x1 121 us: per_device(): lax.psum(jnp.sum(errors, axis=1), ('grp', 'feat')) / total_tokens]
    all_gather x3 -> x0, waiting for transfers between devices: 118 us -> none  [the longest x1 78.8 us: per_device(): sources = lax.all_gather(acts, 'layer', axis=0, tiled=False)]
    dot_general x27 -> x0, matrix products: 87.8 us -> none  [the longest x10 26.7 us: decode_target(): jnp.dot(sources[source], dec_weight[index], preferred_element_type=jnp.fl...]
    reduce_scatter x2 -> x0, waiting for transfers between devices: 26.5 us -> none  [the longest x1 26.5 us: per_device(): lax.psum_scatter(partial.reshape(feat_count * layers * tok_dev, block), '...]
    unnamed x26 -> x7, local copies, waits for them, and re-layouts: 2.11 us -> 19.1 us
  transfers between devices with their start and end apart: 9 -> 0, of which waited for: 4 -> 0; matrix products, arithmetic and copies ran while one was open for 8% -> 0% of each run, Pallas kernels for 0% -> 0%
where the time goes in v1:
time: 186 us
  Pallas kernels  166 us (89%)
  local copies, waits for them, and re-layouts  19.1 us (10%)
    pallas_call x1, Pallas kernels, per_device(): pl.pallas_call(functools.partial(kernel, cfg), out_shape=(jax.ShapeDtypeS...  166 us
    unnamed x7, local copies, waits for them, and re-layouts  19.1 us

profile of v1, /device:TPU:17, one launch (start us, length us, event | category | flops | bytes accessed | tf_op | source)
XLA Modules:
  0.0 185.8 jit_solution(7411457600033922212)
XLA Ops:
  0.6 1.7 copy.12
  2.4 166.1 %transcoder.1 = (bf16[1,1152,2048]{2,1,0:T(8,128)(2,1)}, f32[1,2048]{1,0:T(1,128)}, bf16[5,576,2048]{2,1,0:T(8,128)(2,1)}, f32[4,576]{1,0:T(4,128)}) custom-call(bf16[1,64,2304]{2,1,0:T(8,128)(2,1)} %refs_0_.1, bf16[4,64,576]{2,1,0:T(8,128)(2,1)} %bitcast.7, bf16[1,2304,2048]{2,1,0:T(8,128)(2,1)} %refs_2_.1, f32[1,2048]{1,0:T(1,128)} %refs_3_.1, ...), custom_call_target="tpu_custom_call" | custom-call | tf_op jit(solution)/shard_map/transcoder/pallas_call | solution.py:636
  168.4 5.2 %copy.17 = bf16[1,1152,2048]{2,1,0:T(8,128)(2,1)} copy(bf16[1,1152,2048]{2,1,0:T(8,128)(2,1)} %get-tuple-element.16) | data formatting | bytes 9437184
  173.7 1.3 copy.18
  175.0 0.0 copy-start
  175.0 10.3 %copy.19 = bf16[5,2048,576]{1,2,0:T(8,128)(2,1)} copy(bf16[5,2048,576]{1,2,0:T(8,128)(2,1)} %bitcast.6) | data formatting | bytes 23592960
  185.2 0.0 copy-done
  185.2 0.6 copy.20
Async XLA Ops:
  175.0 10.3 %copy-start = (f32[4,576]{1,0:T(4,128)S(1)}, f32[4,576]{1,0:T(4,128)}, u32[]{:S(2)}) copy-start(f32[4,576]{1,0:T(4,128)} %get-tuple-element.19) | copy-start | bytes 27652

commit v2 on v1

--- a/solution.py
+++ b/solution.py
@@ -118,10 +118,7 @@
             _, dev = peer(k)
             rdma(mine, mine, in_p.at[c, k], in_r.at[c, f], (g, l, dev)).start()
         rdma(mine, mine, in_s.at[c, f], in_r.at[c, f], sdev).start()
-    acc[...] = jnp.zeros_like(acc)
-    dbs[...] = jnp.zeros_like(dbs)
-    ebs[...] = jnp.zeros_like(ebs)
-    for c in range(C):
+    def rows_ready(c):
         for k in range(1, H):
             _, dev = peer(k)
             blk = row_block(c, dev)
@@ -132,11 +129,14 @@
             blk = row_block(c, own)
             rdma(blk, blk, in_s.at[c, own], in_r.at[c, own], sdev).wait_recv()
 
+    dbs[...] = jnp.zeros_like(dbs)
+    ebs[...] = jnp.zeros_like(ebs)
+    acc[0] = jnp.zeros(acc.shape[1:], F32)
+    rows_ready(0)
+
     def cols_copy():
         cols = pl.ds(pl.multiple_of(other * half, half), half)
         return rdma(rows_v.at[:, cols], cols_o, co.at[0], co.at[1], xdev)
-
-    cols_copy().start()
 
     def act_ref(c, s, q):
         return acts.at[s, q, pl.ds(c * R, R), :]
@@ -159,30 +159,47 @@
 
         lax.fori_loop(s, L, one, 0)
 
-    def encode(q, carry):
+    def encode(c, count, q):
+        bias = eb[:, pl.ds(pl.multiple_of(q * cw, cw), cw)]
+        pre = dot_nn(rows_v[pl.ds(c * R, count * R), :], ew_v[q, pl.ds(0, D), :]) + bias
+        acts[l, q, pl.ds(c * R, count * R), :] = jnp.maximum(pre, 0.0).astype(BF)
+
+    def weights_ready(q):
         pltpu.make_async_copy(
             ew.at[0, :, pl.ds(pl.multiple_of(q * cw, cw), cw)], ew_v.at[q, pl.ds(0, D), :], ld_ew.at[q]
         ).wait()
-        bias = eb[:, pl.ds(pl.multiple_of(q * cw, cw), cw)]
-        pre = dot_nn(rows_v[...], ew_v[q, pl.ds(0, D), :]) + bias
-        acts[l, q, pl.ds(0, n), :] = jnp.maximum(pre, 0.0).astype(BF)
+
+    def send_own(c, q):
+        @pl.when(has_r)
+        def _():
+            z_right(c, l, q).start()
+
+        @pl.when(has_l)
+        def _():
+            z_left(c, l, q).start()
+
+        @pl.when(need_s(other, l))
+        def _():
+            x_copy(c, l, q).start()
+
+    def encode_first(q, carry):
+        weights_ready(q)
+        encode(0, 1, q)
         send_own(0, q)
         return carry
 
-    def send_own(c, q):
-        @pl.when(has_r)
-        def _():
-            z_right(c, l, q).start()
-
-        @pl.when(has_l)
-        def _():
-            z_left(c, l, q).start()
-
-        @pl.when(need_s(other, l))
-        def _():
-            x_copy(c, l, q).start()
-
-    lax.fori_loop(0, Q, encode, 0)
+    def encode_second(q, carry):
+        encode(1, 1, q)
+        return carry
+
+    lax.fori_loop(0, Q - 1, encode_first, 0)
+    rows_ready(1)
+    cols_copy().start()
+    lax.fori_loop(0, Q - 1, encode_second, 0)
+    weights_ready(jnp.int32(Q - 1))
+    encode(0, 2, jnp.int32(Q - 1))
+    send_own(0, jnp.int32(Q - 1))
+    acc[1] = jnp.zeros(acc.shape[1:], F32)
     for cp in lw:
         cp.wait()
 
@@ -257,7 +274,7 @@
         r1_copy(c, chip).wait_recv()
         for t in range(L):
             acc[c, t, brow(f, B), :] += (
-                r1r[c, chip, t].astype(F32) + db[pl.ds(t, 1), :] - tgt[t, pl.ds(c * B, B), :].astype(F32)
+                r1r[c, chip, t].astype(F32) + db[pl.ds(t, 1), :] - tgt[pl.ds(c * B, B), t, :].astype(F32)
             )
 
     def mid_err(c):
@@ -484,36 +501,47 @@
     mid_pack(1)
     send_jobs(0, lead, cut(lead + 1))
     mid_sum(1)
-    send_jobs(0, cut(lead + 1), cut(lead + 3))
+    send_jobs(0, cut(lead + 1), cut(lead + 2))
     mid_err(1)
     for k in range(1, F):
         dev = lax.rem(f + k, F)
         rdma(dbs, dbr.at[F - k], db_s.at[k], db_r.at[F - k], (g, l, dev)).start()
-    send_jobs(0, cut(lead + 3), steps)
+    send_jobs(0, cut(lead + 2), cut(lead + 4))
     mid_relay(1)
+    send_jobs(0, cut(lead + 4), steps)
     mid_end(1)
 
+    ahead = jnp.where(jnp.logical_and(has_l, has_r), 0, steps)
+
+    def early(i, carry):
+        send_job(1, i)
+        return carry
+
+    lax.fori_loop(0, ahead, early, 0)
+
     def second(i, carry):
-        send_job(1, i)
+        @pl.when(i >= ahead)
+        def _():
+            send_job(1, i)
 
         @pl.when(jnp.logical_and(i >= 1, i < 1 + Q))
         def _():
             own_job(0, i - 1)
 
-        base = 2 * (i - wait_at)
+        base = 3 * (i - wait_at)
 
         @pl.when(i == wait_at)
         def _():
             wait_others()
 
-        lax.fori_loop(jnp.minimum(jnp.maximum(base, 0), jobs), jnp.minimum(jnp.maximum(base + 2, 0), jobs), grad_job, 0)
+        lax.fori_loop(jnp.minimum(jnp.maximum(base, 0), jobs), jnp.minimum(jnp.maximum(base + 3, 0), jobs), grad_job, 0)
         return carry
 
-    wait_at = min(3, steps - 1)
+    wait_at = min(5, steps - 1)
     lax.fori_loop(0, steps, second, 0)
     for q in range(max(steps - 1, 0), Q):
         own_job(0, jnp.int32(q))
-    lax.fori_loop(min(jobs, 2 * (steps - wait_at)), jobs, grad_job, 0)
+    lax.fori_loop(min(jobs, 3 * (steps - wait_at)), jobs, grad_job, 0)
 
     sums = dbs[...]
     for k in range(1, F):
@@ -648,7 +676,24 @@
             collective_id=0, has_side_effects=True, vmem_limit_bytes=67043328
         ),
         name="transcoder",
-    )(inputs, jnp.swapaxes(targets, 0, 1), enc_weight, enc_bias, jnp.swapaxes(dec_weight, 1, 2), dec_bias)
+    )(inputs, targets, enc_weight, enc_bias, jnp.swapaxes(dec_weight, 1, 2), dec_bias)
+    parts, wide = 2, 8
+
+    def hand_on(enc_ref, dec_ref, enc_out, dec_out):
+        enc_out[...] = enc_ref[...]
+        dec_out[...] = dec_ref[...]
+
+    dec_spec = pl.BlockSpec((1, width // parts, feats), lambda i: (i // parts, i % parts, 0))
+    enc_spec = pl.BlockSpec((1, D // 2 // wide, feats), lambda i: (0, jnp.minimum(i, wide - 1), 0))
+    assert per * parts >= wide
+    enc, dec = pl.pallas_call(
+        hand_on,
+        grid=(per * parts,),
+        out_shape=(jax.ShapeDtypeStruct(enc.shape, BF), jax.ShapeDtypeStruct(dec.shape, BF)),
+        in_specs=[enc_spec, dec_spec],
+        out_specs=(enc_spec, dec_spec),
+        name="hand_on",
+    )(enc, dec)
     return enc, encb, jnp.swapaxes(dec, 1, 2), decb
 
 

time: 186 us -> 176 us (0.946); the launches traced: 186 us -> 174 us
  local copies, waits for them, and re-layouts: 19.1 us -> 1.21 us
  Pallas kernels: 166 us -> 172 us
    unnamed x7 -> x6, local copies, waits for them, and re-layouts: 19.1 us -> 1.21 us
    pallas_call x0 -> x1, Pallas kernels: none -> 14.5 us  [per_device(): pl.pallas_call(hand_on, grid=(per * parts,), out_shape=(jax.ShapeDtypeStr...]
    pallas_call x1, Pallas kernels: 166 us -> 157 us  [per_device(): pl.pallas_call(functools.partial(kernel, cfg), out_shape=(jax.ShapeDtypeS...]
where the time goes in v2:
time: 176 us; the launch traced here: 174 us
  Pallas kernels  172 us (98%)
    pallas_call x1, Pallas kernels, per_device(): pl.pallas_call(functools.partial(kernel, cfg), out_shape=(jax.ShapeDtypeS...  157 us
    pallas_call x1, Pallas kernels, per_device(): pl.pallas_call(hand_on, grid=(per * parts,), out_shape=(jax.ShapeDtypeStr...  14.5 us

profile of v2, /device:TPU:17, one launch (start us, length us, event | category | flops | bytes accessed | tf_op | source)
XLA Modules:
  0.0 173.7 jit_solution(524081524554821872)
XLA Ops:
  0.6 157.3 %transcoder.1 = (bf16[1,1152,2048]{2,1,0:T(8,128)(2,1)}, f32[1,2048]{1,0:T(1,128)}, bf16[5,576,2048]{2,1,0:T(8,128)(2,1)}, f32[4,576]{1,0:T(4,128)}) custom-call(bf16[1,64,2304]{2,1,0:T(8,128)(2,1)} %refs_0_.1, bf16[64,4,576]{2,1,0:T(4,128)(2,1)} %refs_1_.1, bf16[1,2304,2048]{2,1,0:T(8,128)(2,1)} %refs_2_.1, f32[1,2048]{1,0:T(1,128)} %refs_3_.1, ...), custom_call_target="tpu_custom_call" | custom-call | tf_op jit(solution)/shard_map/transcoder/pallas_call | solution.py:664
  158.0 0.0 copy-start.1
  158.0 0.0 copy-start
  158.0 14.5 %hand_on.1 = (bf16[1,1152,2048]{2,1,0:T(8,128)(2,1)}, bf16[5,576,2048]{2,1,0:T(8,128)(2,1)}) custom-call(bf16[1,1152,2048]{2,1,0:T(8,128)(2,1)} %get-tuple-element.10.enc_ref, bf16[5,576,2048]{2,1,0:T(8,128)(2,1)} %get-tuple-element.11.dec_ref), custom_call_target="tpu_custom_call" | custom-call | tf_op jit(solution)/shard_map/hand_on/pallas_call | solution.py:689
  172.5 0.0 copy-done.1
  172.5 0.6 copy.12
  173.1 0.0 copy-done
  173.1 0.6 copy.13
Async XLA Ops:
  158.0 14.5 %copy-start.1 = (f32[1,2048]{1,0:T(1,128)S(1)}, f32[1,2048]{1,0:T(1,128)}, u32[]{:S(2)}) copy-start(f32[1,2048]{1,0:T(1,128)} %get-tuple-element.21) | copy-start | bytes 24580
  158.0 15.1 %copy-start = (f32[4,576]{1,0:T(4,128)S(1)}, f32[4,576]{1,0:T(4,128)}, u32[]{:S(2)}) copy-start(f32[4,576]{1,0:T(4,128)} %get-tuple-element.23) | copy-start | bytes 27652
